TPU v7x, 256 devices: a 2x2x32 block of a 4x8x32 slice. The times are simulated.
256 devices in a mesh: grp: 4 (over y, x), panel: 64 (over z, core).
Axes of the slice: x: 2, y: 2, z: 32, core: 2. Of those that a mesh axis runs over, the one named last changes fastest.
The devices are a block of a 4x8x32 slice.
Arguments:
- density: bfloat16 [8192, 16, 128], P(('grp', 'panel')), parts along dimension 0, may hold values from -6 to 6
- near_blocks: bfloat16 [8192, 8, 128, 128], P(('grp', 'panel')), parts along dimension 0, may hold values from -0.1875 to 0.1875
- neighbours: int32 [8192, 8], P(('grp', 'panel')), parts along dimension 0, may hold values from 0 to 2047, as said below
- counts: int32 [8192], P(('grp', 'panel')), parts along dimension 0, may hold values from 1 to 8, as said below
- coarse_map: int32 [8192], P(('grp', 'panel')), parts along dimension 0, may hold values from 0 to 127, as said below
- restrict: bfloat16 [8192, 128, 128], P(('grp', 'panel')), parts along dimension 0, may hold values from -0.125 to 0.125
- evaluate: bfloat16 [8192, 128, 128], P(('grp', 'panel')), parts along dimension 0, may hold values from -0.5 to 0.5
- coupling: float32 [512, 128], P(('grp', 'panel')), parts along dimension 0, as said below
Outputs:
- potential: bfloat16 [8192, 16, 128], P(('grp', 'panel')), parts along dimension 0
There are 4 independent parts, one for each index of `grp`. A program takes and returns all parts, laid end to end along the dimension named above; each array names one. Nothing has to cross between parts.
Inputs may be any that keep to these rules, and one draw needn't show every extreme that they name: `neighbours`: slot 0 of block b is b itself; every entry lies within 16 blocks of b; in every draw some entry lies exactly 16 blocks below its block and some exactly 16 above. `counts`: every device holds blocks with all 8 slots live. `coarse_map`: block b's coarse cluster is one of the 2 clusters from (b // 32) * 2 on. `coupling`: the matrix is symmetric.
All inputs are finite; a program needn't handle non-finite values.
Results may differ from a plain program's by a relative error of at most 0.0042.
Values may be sent and summed in bfloat16 or wider, within the bound.
A program may use at most 64 MiB of HBM per device.

v0:
```python
import jax
import jax.numpy as jnp
from jax import lax
from jax.sharding import Mesh
from jax.sharding import PartitionSpec as P

PANEL = ("panel_0", "panel_1")
GRP_PANEL = ("grp", "panel_0", "panel_1")


def extended_2(block, sides, width):
    for axis, dim in sides:
        count = lax.axis_size(axis)
        forward = [(i, i + 1) for i in range(count - 1)]
        backward = [(target, source) for source, target in forward]
        low = lax.ppermute(
            lax.slice_in_dim(block, block.shape[dim] - width, None, axis=dim), axis, forward
        )
        high = lax.ppermute(lax.slice_in_dim(block, 0, width, axis=dim), axis, backward)
        block = jnp.concatenate([low, block, high], axis=dim)
    return block


def joined_along(pieces, dim):
    pieces = jnp.moveaxis(pieces, 0, dim)
    lengths = pieces.shape
    return pieces.reshape(*lengths[:dim], lengths[dim] * lengths[dim + 1], *lengths[dim + 2 :])


def gather_in_order(array, axes, order):
    pieces = array[None]
    for k in order:
        pieces = lax.all_gather(pieces, axes[k], axis=0, tiled=True)
    held = [lax.axis_size(axes[k]) for k in reversed(order)]
    pieces = pieces.reshape(*held, *array.shape)
    turned = sorted(range(len(order)), key=lambda place: order[len(order) - 1 - place])
    return pieces.transpose(*turned, *range(len(order), pieces.ndim)).reshape(-1, *array.shape)


def gather_axes(array, axes, order, dim):
    return joined_along(gather_in_order(array, axes, order), dim)


def shards(density, near_blocks, neighbours, counts, coarse_map, restrict, evaluate, coupling):
    blk_count, columns, panels = density.shape
    reach_blocks = blk_count // 2
    anchor = lax.axis_index(PANEL) * blk_count
    extended = extended_2(density, ((PANEL, 0),), reach_blocks)
    local_ids = neighbours - (anchor - reach_blocks)
    picked = jnp.take(extended, local_ids, axis=0)
    slot_ids = jnp.arange(neighbours.shape[1])
    live_slots = slot_ids[None, :] < counts[:, None]
    picked = jnp.where(live_slots[:, :, None, None], picked, jnp.zeros((), jnp.bfloat16))
    near_part = jnp.einsum(
        "bjpq,bjrq->brp", near_blocks, picked, preferred_element_type=jnp.float32
    )
    coarse_dev = coupling.shape[0]
    expand_terms = restrict.shape[1]
    block_terms = jnp.einsum("bkp,brp->brk", restrict, density, preferred_element_type=jnp.float32)
    block_terms = block_terms.reshape(blk_count, columns * expand_terms)
    own_ids = coarse_map - lax.axis_index(PANEL) * coarse_dev
    onehot = (own_ids[None, :] == jnp.arange(coarse_dev)[:, None]).astype(jnp.float32)
    moments = jnp.dot(onehot, block_terms, precision=lax.Precision.HIGHEST)
    all_moments = gather_axes(moments, PANEL, (0, 1), 0)
    local_full = jnp.dot(coupling, all_moments, precision=lax.Precision.HIGHEST)
    local_exp = local_full.astype(jnp.bfloat16)
    spread = jnp.dot(onehot.T.astype(jnp.bfloat16), local_exp, preferred_element_type=jnp.float32)
    spread = spread.astype(jnp.bfloat16).reshape(blk_count, columns, expand_terms)
    far_part = jnp.einsum("bkp,brk->brp", evaluate, spread, preferred_element_type=jnp.float32)
    return (near_part + far_part).astype(jnp.bfloat16)


def solution(mesh):
    torus = Mesh(mesh.devices.reshape(mesh.shape["grp"], 32, 2), ("grp", "panel_0", "panel_1"))
    placed = (
        P(GRP_PANEL, None, None),
        P(GRP_PANEL, None, None, None),
        P(GRP_PANEL, None),
        P(GRP_PANEL),
        P(GRP_PANEL),
        P(GRP_PANEL, None, None),
        P(GRP_PANEL, None, None),
        P(GRP_PANEL, None),
    )
    return jax.shard_map(
        shards, mesh=torus, in_specs=placed, out_specs=P(GRP_PANEL, None, None), check_vma=False
    )
```

profile of v0, /device:TPU:37, one launch (start us, length us, event | category | flops | bytes accessed | tf_op | source)
XLA Modules:
  0.0 128.4 jit_solution(989126953056692734)
XLA Ops:
  6.5 0.0 copy-start
  6.6 0.0 all-gather.4.cloned.1.call-start
  6.6 1.0 fusion.16
  7.5 5.1 %collective-permute-start = (bf16[16,16,128]{2,1,0:T(8,128)(2,1)S(1)}, bf16[16,16,128]{2,1,0:T(8,128)(2,1)S(1)}, u32[]{:S(2)}, u32[]{:S(2)}) collective-permute-start(bf16[16,16,128]{2,1,0:T(8,128)(2,1)S(1)} %get-tuple-element.7), channel_id=1, source_target_pairs={{0,1},{1,2},{2,3},{3,4},{4,5},{5,6},{6,7},{7,8},{8,9},{9,10},{10,1... | collective-permute-start | bytes 196616 | tf_op jit(solution)/shard_map/ppermute | solution.py:16
  12.6 18.6 %collective-permute-start.1 = (bf16[16,16,128]{2,1,0:T(8,128)(2,1)S(1)}, bf16[16,16,128]{2,1,0:T(8,128)(2,1)S(1)}, u32[]{:S(2)}, u32[]{:S(2)}) collective-permute-start(bf16[16,16,128]{2,1,0:T(8,128)(2,1)S(1)} %get-tuple-element.8), channel_id=1, source_target_pairs={{1,0},{2,1},{3,2},{4,3},{5,4},{6,5},{7,6},{8,7},{9,8},{10,9},{11,1... | collective-permute-start | bytes 196616 | tf_op jit(solution)/shard_map/ppermute | solution.py:19
  31.2 0.0 copy-done
  31.2 1.5 %fusion.17 = f32[32,16,128]{2,1,0:T(8,128)S(1)} fusion(bf16[32,16,128]{2,1,0:T(8,128)(2,1)} %param.8, bf16[32,128,128]{2,1,0:T(8,128)(2,1)S(1)} %copy-done), kind=kOutput, calls=%fused_computation.32 | convolution fusion | flops 16777216 | bytes 1441792 | tf_op jit(solution)/shard_map/bkp,brp->brk/dot_general | solution.py:59
  32.8 0.7 broadcast_subtract_fusion
  33.4 0.3 convolution_bitcast_fusion
  33.7 49.7 %all-gather.1 = f32[32,2,2048]{2,1,0:T(2,128)} all-gather(f32[1,2,2048]{2,1,0:T(2,128)S(1)} %convolution_bitcast_fusion), channel_id=2, replica_groups=mesh['grp'=4,'panel_0'=32,'panel_1'=2] {'panel_0'}, dimensions={0}, use_global_device_ids=true | all-gather | bytes 540672 | tf_op jit(solution)/shard_map/all_gather | solution.py:33
  83.4 0.1 all-gather.4.cloned.1.call-update
  83.5 0.7 compare_and_fusion
  84.2 0.1 copy.14
  84.2 0.1 reshape.41
  84.3 0.1 copy.13
  84.4 0.7 iota_compare_fusion.1
  85.1 0.0 copy-start.1
  85.2 0.0 collective-permute-done
  85.2 0.0 collective-permute-done.1
  85.2 0.9 pad_maximum_fusion
  86.1 0.8 gather_fusion
  87.0 4.7 %convolution_bitcast_fusion.1 = f32[32,16,128]{2,1,0:T(8,128)S(1)} fusion(bf16[32,8,128,128]{3,2,1,0:T(8,128)(2,1)} %param.9, bf16[32,8,16,128]{3,2,1,0:T(8,128)(2,1)S(1)} %bitcast.27, pred[32,8]{1,0:T(8,128)(4,1)S(1)} %copy.13, pred[32,8]{1,0:T(8,128)(4,1)S(1)} %iota_compare_fusion.1), kind=kOutput, calls=%fused_computation.5 | convolution fusion | flops 135266304 | bytes 9699840 | tf_op jit(solution)/shard_map/bjpq,bjrq->brp/dot_general | solution.py:54
  91.7 24.6 %all-gather.4.cloned.1.call-done = f32[64,2,2048]{2,1,0:T(2,128)} async-done(((f32[32,2,2048]{2,1,0:T(2,128)}), f32[64,2,2048]{2,1,0:T(2,128)}) %all-gather.4.cloned.1.call-update) | async-done | bytes 1048592 | tf_op jit(solution)/shard_map/all_gather | solution.py:33
  116.3 1.3 %copy.24 = f32[2,32,2,2048]{3,2,0,1:T(2,128)S(1)} copy(f32[2,32,2,2048]{3,2,1,0:T(2,128)} %bitcast.26) | data formatting | bytes 2097152 | tf_op jit(solution)/shard_map/reshape | solution.py:35
  117.6 0.7 reshape_reshape.3
  118.4 0.0 copy-done.1
  118.4 0.7 convolution_convert_fusion.1
  119.0 0.2 fusion.1
  119.3 2.3 %fusion = bf16[32,16,128]{2,1,0:T(8,128)(2,1)} fusion(f32[32,16,128]{2,1,0:T(8,128)S(1)} %convolution_bitcast_fusion.1, bf16[32,16,128]{2,1,0:T(8,128)(2,1)S(1)} %bitcast.29, bf16[32,128,128]{2,1,0:T(8,128)(2,1)} %param.14), kind=kOutput, calls=%fused_computation.6 | convolution fusion | flops 16908288 | bytes 1572864 | tf_op jit(solution)/shard_map/bkp,brk->brp/dot_general | solution.py:69
  (2 shorter events, 0.0 us)
Async XLA Ops:
  6.5 24.7 %copy-start = (bf16[32,128,128]{2,1,0:T(8,128)(2,1)S(1)}, bf16[32,128,128]{2,1,0:T(8,128)(2,1)}, u32[]{:S(2)}) copy-start(bf16[32,128,128]{2,1,0:T(8,128)(2,1)} %param.13) | copy-start | bytes 3145732
  6.6 109.8 %all-gather.4.cloned.1.call-start = ((), (), s32[]{:S(2)}) async-start(), calls=%async_computation | async-start | bytes 1572864 | tf_op jit(solution)/shard_map/all_gather | solution.py:33
  7.5 77.6 %collective-permute-start = (bf16[16,16,128]{2,1,0:T(8,128)(2,1)S(1)}, bf16[16,16,128]{2,1,0:T(8,128)(2,1)S(1)}, u32[]{:S(2)}, u32[]{:S(2)}) collective-permute-start(bf16[16,16,128]{2,1,0:T(8,128)(2,1)S(1)} %get-tuple-element.7), channel_id=1, source_target_pairs={{0,1},{1,2},{2,3},{3,4},{4,5},{5,6},{6,7},{7,8},{8,9},{9,10},{10,1... | collective-permute-start | bytes 196616 | tf_op jit(solution)/shard_map/ppermute | solution.py:16
  12.6 72.5 %collective-permute-start.1 = (bf16[16,16,128]{2,1,0:T(8,128)(2,1)S(1)}, bf16[16,16,128]{2,1,0:T(8,128)(2,1)S(1)}, u32[]{:S(2)}, u32[]{:S(2)}) collective-permute-start(bf16[16,16,128]{2,1,0:T(8,128)(2,1)S(1)} %get-tuple-element.8), channel_id=1, source_target_pairs={{1,0},{2,1},{3,2},{4,3},{5,4},{6,5},{7,6},{8,7},{9,8},{10,9},{11,1... | collective-permute-start | bytes 196616 | tf_op jit(solution)/shard_map/ppermute | solution.py:19
  85.1 33.2 %copy-start.1 = (f32[2,128]{1,0:T(2,128)S(1)}, f32[2,128]{1,0:T(2,128)}, u32[]{:S(2)}) copy-start(f32[2,128]{1,0:T(2,128)} %param.15) | copy-start | bytes 3076
Sparse Core Ops, SparseCore 0:
  83.6 32.6 all-gather.3
where the time goes:
time: 129 us; the launch traced here: 128 us
  blocking collectives  49.7 us (39%)
  waiting for transfers between devices  24.7 us (19%)
  starting transfers between devices  23.7 us (18%)
  between operations  13.5 us (10%)
  matrix products  9.67 us (7%)
  local copies, waits for them, and re-layouts  4.13 us (3%)
  other arithmetic  3.06 us (2%)
    all_gather x1, blocking collectives, gather_in_order(): pieces = lax.all_gather(pieces, axes[k], axis=0, tiled=True)  49.7 us
    all_gather x1, waiting for transfers between devices, gather_in_order(): pieces = lax.all_gather(pieces, axes[k], axis=0, tiled=True)  24.6 us
    ppermute x1, starting transfers between devices, extended_2(): lax.ppermute(lax.slice_in_dim(block, 0, width, axis=dim), axis, backward)  18.6 us
    ppermute x1, starting transfers between devices, extended_2(): lax.ppermute(lax.slice_in_dim(block, block.shape[dim] - width, None, axis...  5.09 us
    dot_general x1, matrix products, shards(): jnp.einsum('bjpq,bjrq->brp', near_blocks, picked, preferred_element_type=...  4.7 us
  transfers between devices with their start and end apart: 3, of which 1 were waited for; matrix products, arithmetic and copies ran while one was open for 8% of the time, Pallas kernels for 0%

commit v1 on v0

--- a/solution.py
+++ b/solution.py
@@ -30,7 +30,9 @@
 def gather_in_order(array, axes, order):
     pieces = array[None]
     for k in order:
-        pieces = lax.all_gather(pieces, axes[k], axis=0, tiled=True)
+        pieces = jnp.concatenate(
+            lax.all_to_all(jnp.stack([pieces] * lax.axis_size(axes[k])), axes[k], 0, 0), axis=0
+        )
     held = [lax.axis_size(axes[k]) for k in reversed(order)]
     pieces = pieces.reshape(*held, *array.shape)
     turned = sorted(range(len(order)), key=lambda place: order[len(order) - 1 - place])

time: 129 us -> 112 us (0.87)
  blocking collectives: 49.7 us -> 6.77 us
  waiting for transfers between devices: 24.7 us -> 48 us
  starting transfers between devices: 23.7 us -> 38.9 us
  between operations: 13.5 us -> 0.11 us
    all_gather x1 -> x0, blocking collectives: 49.7 us -> none  [gather_in_order(): pieces = lax.all_gather(pieces, axes[k], axis=0, tiled=True)]
    all_to_all x0 -> x1, starting transfers between devices: none -> 33.2 us  [gather_in_order(): lax.all_to_all(jnp.stack([pieces] * lax.axis_size(axes[k])), axes[k], 0, 0)]
    all_gather x1 -> x0, waiting for transfers between devices: 24.6 us -> none  [gather_in_order(): pieces = lax.all_gather(pieces, axes[k], axis=0, tiled=True)]
    ppermute x1, waiting for transfers between devices: 0.01 us -> 22.3 us  [extended_2(): lax.ppermute(lax.slice_in_dim(block, block.shape[dim] - width, None, axis...]
    ppermute x1, starting transfers between devices: 18.6 us -> 1.95 us  [extended_2(): lax.ppermute(lax.slice_in_dim(block, 0, width, axis=dim), axis, backward)]
    ppermute x1, waiting for transfers between devices: 0.01 us -> 13.4 us  [extended_2(): lax.ppermute(lax.slice_in_dim(block, 0, width, axis=dim), axis, backward)]
    all_to_all x0 -> x1, waiting for transfers between devices: none -> 12.3 us  [gather_in_order(): lax.all_to_all(jnp.stack([pieces] * lax.axis_size(axes[k])), axes[k], 0, 0)]
    all_to_all x0 -> x1, blocking collectives: none -> 6.77 us  [gather_in_order(): lax.all_to_all(jnp.stack([pieces] * lax.axis_size(axes[k])), axes[k], 0, 0)]
  transfers between devices with their start and end apart: 3 -> 3, of which waited for: 1 -> 3; matrix products, arithmetic and copies ran while one was open for 8% -> 8% of each run, Pallas kernels for 0% -> 0%
where the time goes in v1:
time: 112 us; the launch traced here: 111 us
  waiting for transfers between devices  48 us (43%)
  starting transfers between devices  38.9 us (35%)
  matrix products  9.68 us (9%)
  blocking collectives  6.77 us (6%)
  local copies, waits for them, and re-layouts  4.35 us (4%)
  other arithmetic  3.6 us (3%)
    all_to_all x1, starting transfers between devices, gather_in_order(): lax.all_to_all(jnp.stack([pieces] * lax.axis_size(axes[k])), axes[k], 0, 0)  33.2 us
    ppermute x1, waiting for transfers between devices, extended_2(): lax.ppermute(lax.slice_in_dim(block, block.shape[dim] - width, None, axis...  22.3 us
    ppermute x1, waiting for transfers between devices, extended_2(): lax.ppermute(lax.slice_in_dim(block, 0, width, axis=dim), axis, backward)  13.4 us
    all_to_all x1, waiting for transfers between devices, gather_in_order(): lax.all_to_all(jnp.stack([pieces] * lax.axis_size(axes[k])), axes[k], 0, 0)  12.3 us
    all_to_all x1, blocking collectives, gather_in_order(): lax.all_to_all(jnp.stack([pieces] * lax.axis_size(axes[k])), axes[k], 0, 0)  6.77 us
    dot_general x1, matrix products, shards(): jnp.einsum('bjpq,bjrq->brp', near_blocks, picked, preferred_element_type=...  4.7 us
    ppermute x1, starting transfers between devices, extended_2(): lax.ppermute(lax.slice_in_dim(block, block.shape[dim] - width, None, axis...  3.76 us
    dot_general x1, matrix products, shards(): jnp.einsum('bkp,brk->brp', evaluate, spread, preferred_element_type=jnp.f...  2.28 us
  transfers between devices with their start and end apart: 3, of which 3 were waited for; matrix products, arithmetic and copies ran while one was open for 8% of the time, Pallas kernels for 0%

profile of v1, /device:TPU:37, one launch (start us, length us, event | category | flops | bytes accessed | tf_op | source)
XLA Modules:
  0.0 111.4 jit_solution(16117069117862113670)
XLA Ops:
  0.0 0.0 copy-start
  0.0 0.7 broadcast_subtract_fusion
  0.8 0.5 copy-done
  1.2 1.5 %fusion.18 = f32[32,16,128]{2,1,0:T(8,128)S(1)} fusion(bf16[32,16,128]{2,1,0:T(8,128)(2,1)} %param.8, bf16[32,128,128]{2,1,0:T(8,128)(2,1)S(1)} %copy-done), kind=kOutput, calls=%fused_computation.32 | convolution fusion | flops 16777216 | bytes 1441792 | tf_op jit(solution)/shard_map/bkp,brp->brk/dot_general | solution.py:61
  2.8 0.3 fusion.8
  3.1 1.0 stack.6
  4.1 33.2 %all-to-all-start = ((f32[32,1,2,2048]{3,2,1,0:T(2,128)}), f32[32,1,2,2048]{3,2,1,0:T(2,128)S(1)}, u32[]{:S(2)}, u32[]{:S(2)}) async-start(f32[32,1,2,2048]{3,2,1,0:T(2,128)} %stack.6), calls=%async_computation | async-start | bytes 1048576 | tf_op jit(solution)/shard_map/all_to_all | solution.py:34
  37.3 0.9 fusion.17
  38.2 3.8 %collective-permute-start = (bf16[16,16,128]{2,1,0:T(8,128)(2,1)S(1)}, bf16[16,16,128]{2,1,0:T(8,128)(2,1)S(1)}, u32[]{:S(2)}, u32[]{:S(2)}) collective-permute-start(bf16[16,16,128]{2,1,0:T(8,128)(2,1)S(1)} %get-tuple-element.7), channel_id=1, source_target_pairs={{0,1},{1,2},{2,3},{3,4},{4,5},{5,6},{6,7},{7,8},{8,9},{9,10},{10,1... | collective-permute-start | bytes 196616 | tf_op jit(solution)/shard_map/ppermute | solution.py:16
  42.0 2.0 %collective-permute-start.1 = (bf16[16,16,128]{2,1,0:T(8,128)(2,1)S(1)}, bf16[16,16,128]{2,1,0:T(8,128)(2,1)S(1)}, u32[]{:S(2)}, u32[]{:S(2)}) collective-permute-start(bf16[16,16,128]{2,1,0:T(8,128)(2,1)S(1)} %get-tuple-element.8), channel_id=1, source_target_pairs={{1,0},{2,1},{3,2},{4,3},{5,4},{6,5},{7,6},{8,7},{9,8},{10,9},{11,1... | collective-permute-start | bytes 196616 | tf_op jit(solution)/shard_map/ppermute | solution.py:19
  43.9 0.7 compare_and_fusion
  44.6 0.1 copy.13
  44.7 0.1 reshape.39
  44.8 0.1 copy.12
  44.9 0.7 iota_compare_fusion.1
  45.6 22.3 %collective-permute-done = bf16[16,16,128]{2,1,0:T(8,128)(2,1)S(1)} collective-permute-done((bf16[16,16,128]{2,1,0:T(8,128)(2,1)S(1)}, bf16[16,16,128]{2,1,0:T(8,128)(2,1)S(1)}, u32[]{:S(2)}, u32[]{:S(2)}) %collective-permute-start) | collective-permute-done | bytes 65568 | tf_op jit(solution)/shard_map/ppermute | solution.py:16
  67.9 13.4 %collective-permute-done.1 = bf16[16,16,128]{2,1,0:T(8,128)(2,1)S(1)} collective-permute-done((bf16[16,16,128]{2,1,0:T(8,128)(2,1)S(1)}, bf16[16,16,128]{2,1,0:T(8,128)(2,1)S(1)}, u32[]{:S(2)}, u32[]{:S(2)}) %collective-permute-start.1) | collective-permute-done | bytes 65568 | tf_op jit(solution)/shard_map/ppermute | solution.py:19
  81.3 0.9 pad_maximum_fusion.1
  82.2 0.9 gather_fusion
  83.1 0.0 copy-start.1
  83.1 4.7 %convolution_bitcast_fusion = f32[32,16,128]{2,1,0:T(8,128)S(1)} fusion(bf16[32,8,128,128]{3,2,1,0:T(8,128)(2,1)} %param.9, bf16[32,8,16,128]{3,2,1,0:T(8,128)(2,1)S(1)} %bitcast.23, pred[32,8]{1,0:T(8,128)(4,1)S(1)} %copy.12, pred[32,8]{1,0:T(8,128)(4,1)S(1)} %iota_compare_fusion.1), kind=kOutput, calls=%fused_computation.4 | convolution fusion | flops 135266304 | bytes 9699840 | tf_op jit(solution)/shard_map/bjpq,bjrq->brp/dot_general | solution.py:56
  87.8 12.3 %all-to-all-done = f32[32,1,2,2048]{3,2,1,0:T(2,128)S(1)} async-done(((f32[32,1,2,2048]{3,2,1,0:T(2,128)}), f32[32,1,2,2048]{3,2,1,0:T(2,128)S(1)}, u32[]{:S(2)}, u32[]{:S(2)}) %all-to-all-start) | async-done | bytes 524320 | tf_op jit(solution)/shard_map/all_to_all | solution.py:34
  100.1 0.5 pad_maximum_fusion
  100.6 6.8 %all_to_all.10 = f32[2,32,2,2048]{3,2,1,0:T(2,128)S(1)} all-to-all(f32[2,32,2,2048]{3,2,1,0:T(2,128)S(1)} %pad_maximum_fusion), channel_id=1, replica_groups=mesh['grp'=4,'panel_0'=32,'panel_1'=2] {'panel_1'}, dimensions={0} | all-to-all | bytes 2097152 | tf_op jit(solution)/shard_map/all_to_all | solution.py:34
  107.4 0.1 copy.14
  107.5 0.7 reshape_reshape.3
  108.2 0.0 copy-done.1
  108.2 0.7 convolution_convert_fusion.1
  108.8 0.2 fusion.1
  109.1 2.3 %fusion = bf16[32,16,128]{2,1,0:T(8,128)(2,1)} fusion(f32[32,16,128]{2,1,0:T(8,128)S(1)} %convolution_bitcast_fusion, bf16[32,16,128]{2,1,0:T(8,128)(2,1)S(1)} %bitcast.25, bf16[32,128,128]{2,1,0:T(8,128)(2,1)} %param.14), kind=kOutput, calls=%fused_computation.5 | convolution fusion | flops 16908288 | bytes 1572864 | tf_op jit(solution)/shard_map/bkp,brk->brp/dot_general | solution.py:71
  (2 shorter events, 0.0 us)
Async XLA Ops:
  0.0 1.2 %copy-start = (bf16[32,128,128]{2,1,0:T(8,128)(2,1)S(1)}, bf16[32,128,128]{2,1,0:T(8,128)(2,1)}, u32[]{:S(2)}) copy-start(bf16[32,128,128]{2,1,0:T(8,128)(2,1)} %param.13) | copy-start | bytes 3145732
  4.1 96.0 %all-to-all-start = ((f32[32,1,2,2048]{3,2,1,0:T(2,128)}), f32[32,1,2,2048]{3,2,1,0:T(2,128)S(1)}, u32[]{:S(2)}, u32[]{:S(2)}) async-start(f32[32,1,2,2048]{3,2,1,0:T(2,128)} %stack.6), calls=%async_computation | async-start | bytes 1048576 | tf_op jit(solution)/shard_map/all_to_all | solution.py:34
  38.2 29.7 %collective-permute-start = (bf16[16,16,128]{2,1,0:T(8,128)(2,1)S(1)}, bf16[16,16,128]{2,1,0:T(8,128)(2,1)S(1)}, u32[]{:S(2)}, u32[]{:S(2)}) collective-permute-start(bf16[16,16,128]{2,1,0:T(8,128)(2,1)S(1)} %get-tuple-element.7), channel_id=1, source_target_pairs={{0,1},{1,2},{2,3},{3,4},{4,5},{5,6},{6,7},{7,8},{8,9},{9,10},{10,1... | collective-permute-start | bytes 196616 | tf_op jit(solution)/shard_map/ppermute | solution.py:16
  42.0 39.3 %collective-permute-start.1 = (bf16[16,16,128]{2,1,0:T(8,128)(2,1)S(1)}, bf16[16,16,128]{2,1,0:T(8,128)(2,1)S(1)}, u32[]{:S(2)}, u32[]{:S(2)}) collective-permute-start(bf16[16,16,128]{2,1,0:T(8,128)(2,1)S(1)} %get-tuple-element.8), channel_id=1, source_target_pairs={{1,0},{2,1},{3,2},{4,3},{5,4},{6,5},{7,6},{8,7},{9,8},{10,9},{11,1... | collective-permute-start | bytes 196616 | tf_op jit(solution)/shard_map/ppermute | solution.py:19
  83.1 25.1 %copy-start.1 = (f32[2,128]{1,0:T(2,128)S(1)}, f32[2,128]{1,0:T(2,128)}, u32[]{:S(2)}) copy-start(f32[2,128]{1,0:T(2,128)} %param.15) | copy-start | bytes 3076
